TPU v7x, 32 devices: a whole 2x2x4 slice. The times are simulated.
32 devices in a mesh: group: 4 (over y, x), expert: 4 (over z), dp: 2 (over core).
Axes of the slice: x: 2, y: 2, z: 4, core: 2. Of those that a mesh axis runs over, the one named last changes fastest.
Arguments:
- tokens: bfloat16 [8, 16, 7168], P(('expert', 'dp'), 'group'), may hold values from -6 to 6
- expert_ids: int32 [8, 16, 8], P(('expert', 'dp')), may hold values from 0 to 31, as said below
- gate_codes: int32 [8, 16, 8], P(('expert', 'dp')), may hold values from 1 to 1023
- w_gate: bfloat16 [4, 7168, 2048], P('expert', None, 'group'), may hold values from -0.0625 to 0.0625
- w_up: bfloat16 [4, 7168, 2048], P('expert', None, 'group'), may hold values from -0.0625 to 0.0625
- w_down: bfloat16 [4, 2048, 7168], P('expert', 'group'), may hold values from -0.125 to 0.125
Outputs:
- mixed: bfloat16 [8, 16, 7168], P(('expert', 'dp'), 'group')
Inputs may be any that keep to these rules, and one draw needn't show every extreme that they name: `expert_ids`: each token names 8 different experts, all within at most 4 of the 8 groups of 4 consecutive ids. In every set (one index of the first dimension), each expert below 4 is named by at most 4 tokens, and some expert by exactly 4; a token names at most 4 experts below 4.
All inputs are finite; a program needn't handle non-finite values.
Results may differ from a plain program's by a relative error of at most 0.015.
Values may be sent and summed in bfloat16 or wider, within the bound.
A program may use at most 64 MiB of HBM per device.

v0:
```python
import jax
import jax.numpy as jnp
from jax import lax
from jax.sharding import PartitionSpec as P

CAPG = 4


def routing(expert_ids, gate_codes, experts, capacity):
    codes = gate_codes.astype(jnp.float32)
    gates = 2.5 * codes / jnp.sum(codes, axis=-1, keepdims=True)
    window = jnp.arange(experts, dtype=jnp.int32)
    hits = expert_ids[..., None] == window
    member = jnp.any(hits, axis=-2).astype(jnp.int32)
    weight = jnp.sum(jnp.where(hits, gates[..., None], jnp.float32(0.0)), axis=-2)
    rank = jnp.cumsum(member, axis=-2) - member
    slots = jnp.arange(capacity, dtype=jnp.int32)
    place = (member[..., None] == 1) & (rank[..., None] == slots)
    return (place, weight)


def per_device(tokens, expert_ids, gate_codes, w_gate, w_up, w_down):
    experts = lax.axis_size("expert")
    gathered = lax.all_gather(tokens, "group", axis=1, tiled=True)
    place, weight = routing(expert_ids[0], gate_codes[0], experts, CAPG)
    pick = place.astype(jnp.bfloat16)
    rows = jnp.einsum("tej,td->ejd", pick, gathered[0], preferred_element_type=jnp.float32).astype(
        jnp.bfloat16
    )
    mix = jnp.where(place, weight[..., None], jnp.float32(0.0))
    slot_rows = lax.all_to_all(rows, "expert", split_axis=0, concat_axis=0, tiled=True)
    count = slot_rows.shape[0] * slot_rows.shape[1]
    flat = slot_rows.reshape(count, slot_rows.shape[2])
    first = jnp.dot(flat, w_gate[0], preferred_element_type=jnp.float32)
    second = jnp.dot(flat, w_up[0], preferred_element_type=jnp.float32)
    hidden = (jax.nn.silu(first) * second).astype(jnp.bfloat16)
    partial_value = jnp.dot(hidden, w_down[0], preferred_element_type=jnp.float32).astype(
        jnp.bfloat16
    )
    partial_value = partial_value.reshape(slot_rows.shape)
    returned = lax.all_to_all(partial_value, "expert", split_axis=0, concat_axis=0, tiled=True)
    mixed = lax.psum_scatter(
        jnp.einsum(
            "tej,ejd->td",
            mix,
            returned,
            precision=lax.Precision.HIGHEST,
            preferred_element_type=jnp.float32,
        ),
        "group",
        scatter_dimension=0,
        tiled=True,
    ).astype(jnp.bfloat16)
    return mixed[None]


def solution(mesh):
    placed = (
        P(("expert", "dp"), "group", None),
        P(("expert", "dp"), None, None),
        P(("expert", "dp"), None, None),
        P("expert", None, "group"),
        P("expert", None, "group"),
        P("expert", "group", None),
    )
    return jax.shard_map(
        per_device,
        mesh=mesh,
        in_specs=placed,
        out_specs=P(("expert", "dp"), "group", None),
        check_vma=False,
    )
```

profile of v0, /device:TPU:0, one launch (start us, length us, event | category | flops | bytes accessed | tf_op | source)
XLA Modules:
  0.0 71.0 jit_solution(4581703472650976973)
XLA Ops:
  0.0 0.7 fusion.22
  0.7 0.1 copy.21
  0.9 0.1 copy.23
  0.9 0.1 copy.22
  1.0 0.9 %copy.24 = bf16[1,4,7168]{2,0,1:T(2,128)(2,1)S(1)} copy(bf16[1,4,7168]{2,1,0:T(4,128)(2,1)} %param.6) | data formatting | bytes 114688 | tf_op args[0]
  2.0 11.3 %all_gather.3 = bf16[1,16,7168]{2,0,1:T(2,128)(2,1)S(1)} all-gather(bf16[1,4,7168]{2,0,1:T(2,128)(2,1)S(1)} %copy.24), channel_id=1, replica_groups=mesh['group'=4,'expert'=4,'dp'=2] {'group'}, dimensions={1}, use_global_device_ids=true | all-gather | bytes 286720 | tf_op jit(solution)/shard_map/all_gather | solution.py:24
  13.2 0.2 convolution_convert_fusion.1
  13.4 11.6 %all_to_all.10 = bf16[4,4,7168]{2,1,0:T(4,128)(2,1)S(1)} all-to-all(bf16[4,4,7168]{2,1,0:T(4,128)(2,1)S(1)} %convolution_convert_fusion.1), channel_id=1, replica_groups=mesh['group'=4,'expert'=4,'dp'=2] {'expert'}, dimensions={0} | all-to-all | bytes 458752 | tf_op jit(solution)/shard_map/all_to_all | solution.py:31
  25.0 0.1 reshape.49
  25.0 4.1 %fusion.3 = f32[16,512]{1,0:T(8,128)S(1)} fusion(bf16[16,7168]{1,0:T(8,128)(2,1)S(1)} %reshape.49, bf16[1,7168,512]{2,1,0:T(8,128)(2,1)} %param.9), kind=kOutput, calls=%fused_computation.6 | convolution fusion | flops 117440512 | bytes 7602176 | tf_op jit(solution)/shard_map/dot_general | solution.py:34
  29.2 0.0 copy-start
  29.2 0.0 copy-start.2
  29.2 0.0 copy-start.1
  29.2 7.3 %convolution_convert_fusion = bf16[16,7168]{1,0:T(8,128)(2,1)S(1)} fusion(bf16[1,512,7168]{2,1,0:T(8,128)(2,1)} %param.11, bf16[16,7168]{1,0:T(8,128)(2,1)S(1)} %reshape.49, bf16[1,7168,512]{2,1,0:T(8,128)(2,1)} %param.10, f32[16,512]{1,0:T(8,128)S(1)} %fusion.3), kind=kOutput, calls=%fused_computation.1 | convolution fusion | flops 235044864 | bytes 15171584 | tf_op jit(solution)/shard_map/dot_general | solution.py:37
  36.5 0.8 %reshape.50 = bf16[4,4,7168]{2,1,0:T(4,128)(2,1)} reshape(bf16[16,7168]{1,0:T(8,128)(2,1)S(1)} %convolution_convert_fusion) | data formatting | bytes 458752 | tf_op jit(solution)/shard_map/reshape | solution.py:40
  37.3 3.4 %all-to-all-start.1 = ((bf16[4,4,7168]{2,1,0:T(4,128)(2,1)}), bf16[4,4,7168]{2,1,0:T(4,128)(2,1)S(1)}, u32[]{:S(2)}, u32[]{:S(2)}) async-start(bf16[4,4,7168]{2,1,0:T(4,128)(2,1)} %reshape.50), calls=%async_computation.1 | async-start | bytes 458752 | tf_op jit(solution)/shard_map/all_to_all | solution.py:41
  40.7 0.0 copy-done
  40.7 0.0 copy-done.2
  40.7 0.6 dynamic-slice
  42.0 0.0 copy-done.1
  42.0 5.2 %all-to-all-done.1 = bf16[4,4,7168]{2,1,0:T(4,128)(2,1)S(1)} async-done(((bf16[4,4,7168]{2,1,0:T(4,128)(2,1)}), bf16[4,4,7168]{2,1,0:T(4,128)(2,1)S(1)}, u32[]{:S(2)}, u32[]{:S(2)}) %all-to-all-start.1) | async-done | bytes 229408 | tf_op jit(solution)/shard_map/all_to_all | solution.py:41
  47.1 0.4 convolution_bitcast_fusion
  47.6 22.7 %all-reduce.2 = bf16[16,7168]{1,0:T(8,128)(2,1)S(1)} all-reduce(f32[16,7168]{1,0:T(8,128)S(1)} %convolution_bitcast_fusion), channel_id=2, replica_groups=mesh['group'=4,'expert'=4,'dp'=2] {'group'}, use_global_device_ids=true, to_apply=%region_4.5.clone | all-reduce | flops 114688 | bytes 688128
  70.3 0.7 fusion.15
  (6 shorter events, 0.1 us)
Async XLA Ops:
  29.2 11.5 %copy-start = (s32[1,16,8]{1,2,0:T(8,128)S(1)}, s32[1,16,8]{1,2,0:T(8,128)}, u32[]{:S(2)}) copy-start(s32[1,16,8]{1,2,0:T(8,128)} %param.8) | copy-start | bytes 1540
  29.2 11.5 %copy-start.2 = (u32[32]{0:T(128)S(1)}, u32[32]{0:T(128)}, u32[]{:S(2)}) copy-start(u32[32]{0:T(128)} %constant.23) | copy-start | bytes 388
  29.2 12.8 %copy-start.1 = (s32[1,16,8]{1,2,0:T(8,128)S(1)}, s32[1,16,8]{1,2,0:T(8,128)}, u32[]{:S(2)}) copy-start(s32[1,16,8]{1,2,0:T(8,128)} %param.7) | copy-start | bytes 1540
  37.3 9.9 %all-to-all-start.1 = ((bf16[4,4,7168]{2,1,0:T(4,128)(2,1)}), bf16[4,4,7168]{2,1,0:T(4,128)(2,1)S(1)}, u32[]{:S(2)}, u32[]{:S(2)}) async-start(bf16[4,4,7168]{2,1,0:T(4,128)(2,1)} %reshape.50), calls=%async_computation.1 | async-start | bytes 458752 | tf_op jit(solution)/shard_map/all_to_all | solution.py:41
where the time goes:
time: 71.3 us; the launch traced here: 71 us
  blocking collectives  45.5 us (64%)
  matrix products  12.1 us (17%)
  waiting for transfers between devices  5.15 us (7%)
  starting transfers between devices  3.38 us (5%)
  local copies, waits for them, and re-layouts  3.28 us (5%)
  other arithmetic  0.8 us (1%)
  between operations  0.74 us (1%)
    unnamed x1, blocking collectives  22.7 us
    all_to_all x1, blocking collectives, per_device(): lax.all_to_all(rows, 'expert', split_axis=0, concat_axis=0, tiled=True)  11.6 us
    all_gather x1, blocking collectives, per_device(): gathered = lax.all_gather(tokens, 'group', axis=1, tiled=True)  11.3 us
    dot_general x1, matrix products, per_device(): jnp.dot(hidden, w_down[0], preferred_element_type=jnp.float32)  7.31 us
    all_to_all x1, waiting for transfers between devices, per_device(): lax.all_to_all(partial_value, 'expert', split_axis=0, concat_axis=0, tile...  5.15 us
    dot_general x1, matrix products, per_device(): first = jnp.dot(flat, w_gate[0], preferred_element_type=jnp.float32)  4.13 us
    all_to_all x1, starting transfers between devices, per_device(): lax.all_to_all(partial_value, 'expert', split_axis=0, concat_axis=0, tile...  3.38 us
    unnamed x8, local copies, waits for them, and re-layouts  1.51 us
  transfers between devices with their start and end apart: 1, of which 1 were waited for; matrix products, arithmetic and copies ran while one was open for 1% of the time, Pallas kernels for 0%

commit v1 on v0

v1 whole, which is shorter than its diff:
```python
import functools

import jax
import jax.numpy as jnp
from jax import lax
from jax.experimental import pallas as pl
from jax.experimental.pallas import tpu as pltpu
from jax.sharding import PartitionSpec as P

CAPG = 4
CHUNKS = 4
MESH = pl.DeviceIdType.MESH


def dot(a, b):
    return jnp.dot(a, b, preferred_element_type=jnp.float32)


def routing(ids, codes, experts, capacity):
    tokens = ids.shape[0]
    wide = experts * capacity
    codes = codes.astype(jnp.float32)
    gates = 2.5 * codes / jnp.sum(codes, axis=-1, keepdims=True)
    lane = lax.broadcasted_iota(jnp.int32, (tokens, wide), 1)
    member = jnp.zeros((tokens, wide), jnp.float32)
    weight = jnp.zeros((tokens, wide), jnp.float32)
    for e in range(experts):
        hits = ids == e
        named = jnp.max(jnp.where(hits, 1.0, 0.0), axis=-1, keepdims=True)
        gate = jnp.sum(jnp.where(hits, gates, 0.0), axis=-1, keepdims=True)
        mine = (lane >= e * capacity) & (lane < (e + 1) * capacity)
        member = jnp.where(mine, named, member)
        weight = jnp.where(mine, gate, weight)
    row = lax.broadcasted_iota(jnp.int32, (tokens, tokens), 0)
    column = lax.broadcasted_iota(jnp.int32, (tokens, tokens), 1)
    before = jnp.where(column < row, 1.0, 0.0).astype(jnp.bfloat16)
    rank = dot(before, member.astype(jnp.bfloat16))
    slot = (lane % capacity).astype(jnp.float32)
    place = jnp.where(rank == slot, member, 0.0)
    mix = place * weight
    row = lax.broadcasted_iota(jnp.int32, (wide, wide), 0)
    column = lax.broadcasted_iota(jnp.int32, (wide, wide), 1)
    eye = jnp.where(column == row, 1.0, 0.0).astype(jnp.bfloat16)
    pick = lax.dot_general(
        eye,
        place.astype(jnp.bfloat16),
        (((1,), (1,)), ((), ())),
        preferred_element_type=jnp.float32,
    )
    return pick.astype(jnp.bfloat16), mix


def kernel(
    groups, experts, tokens, ids, codes, w_gate, w_up, w_down, out,
    tok, ids_v, codes_v, wg, wu, wd, rows, slots, part, ret, mixed, red,
    in_sem, w_sem, ga_s, ga_r, di_s, di_r, re_s, re_r, sc_s, sc_r,
):
    g = lax.axis_index("group")
    z = lax.axis_index("expert")
    own = tokens.shape[0]
    width = tokens.shape[1]
    size = width // CHUNKS
    cuts = [pl.ds(c * size, size) for c in range(CHUNKS)]
    cap = CAPG

    tok_in = pltpu.make_async_copy(tokens, tok.at[g], in_sem.at[0])
    ids_in = pltpu.make_async_copy(ids, ids_v, in_sem.at[1])
    codes_in = pltpu.make_async_copy(codes, codes_v, in_sem.at[2])
    tok_in.start()
    ids_in.start()
    codes_in.start()

    barrier = pltpu.get_barrier_semaphore()
    group_peers = [lax.rem(g + k, groups) for k in range(1, groups)]
    expert_peers = [lax.rem(z + k, experts) for k in range(1, experts)]
    for peer in group_peers:
        pl.semaphore_signal(barrier, inc=1, device_id={"group": peer}, device_id_type=MESH)
    for peer in expert_peers:
        pl.semaphore_signal(barrier, inc=1, device_id={"expert": peer}, device_id_type=MESH)

    gate_in = [pltpu.make_async_copy(w_gate.at[cut, :], wg.at[cut, :], w_sem.at[0, c]) for c, cut in enumerate(cuts)]
    up_in = [pltpu.make_async_copy(w_up.at[cut, :], wu.at[cut, :], w_sem.at[1, c]) for c, cut in enumerate(cuts)]
    down_in = [pltpu.make_async_copy(w_down.at[:, cut], wd.at[:, cut], w_sem.at[2, c]) for c, cut in enumerate(cuts)]
    for c in range(CHUNKS):
        gate_in[c].start()
        up_in[c].start()
    for c in range(CHUNKS):
        down_in[c].start()

    ids_in.wait()
    codes_in.wait()
    pick, mix = routing(ids_v[...], codes_v[...], experts, cap)
    mix_hi = mix.astype(jnp.bfloat16)
    mix_lo = (mix - mix_hi.astype(jnp.float32)).astype(jnp.bfloat16)
    tok_in.wait()
    pl.semaphore_wait(barrier, groups + experts - 2)

    def remote(axis, peer, src, dst, send, recv):
        return pltpu.make_async_remote_copy(
            src_ref=src, dst_ref=dst, send_sem=send, recv_sem=recv,
            device_id={axis: peer}, device_id_type=MESH,
        )

    gather = [
        [
            remote("group", peer, tok.at[g, :, cut], tok.at[g, :, cut], ga_s.at[c, k], ga_r.at[c, k])
            for k, peer in enumerate(group_peers)
        ]
        for c, cut in enumerate(cuts)
    ]
    dispatch = [
        [
            remote("expert", peer, rows.at[peer, :, cut], slots.at[z, :, cut], di_s.at[c, k], di_r.at[c, k])
            for k, peer in enumerate(expert_peers)
        ]
        for c, cut in enumerate(cuts)
    ]
    giveback = [
        [
            remote("expert", peer, part.at[peer, :, cut], ret.at[z, :, cut], re_s.at[c, k], re_r.at[c, k])
            for k, peer in enumerate(expert_peers)
        ]
        for c, cut in enumerate(cuts)
    ]
    scatter = [
        [
            remote("group", peer, mixed.at[peer, :, cut], red.at[g, :, cut], sc_s.at[c, k], sc_r.at[c, k])
            for k, peer in enumerate(group_peers)
        ]
        for c, cut in enumerate(cuts)
    ]

    for c in range(CHUNKS):
        for copy in gather[c]:
            copy.start()
    for c, cut in enumerate(cuts):
        for copy in gather[c]:
            copy.wait_recv()
        chosen = dot(pick, tok[:, :, cut].reshape(groups * own, size)).astype(jnp.bfloat16)
        rows[:, :, cut] = chosen.reshape(experts, cap, size)
        for copy in dispatch[c]:
            copy.start()
        slots[z, :, cut] = rows[z, :, cut]

    first = second = None
    for c, cut in enumerate(cuts):
        for copy in dispatch[c]:
            copy.wait_recv()
        gate_in[c].wait()
        up_in[c].wait()
        flat = slots[:, :, cut].reshape(experts * cap, size)
        a = dot(flat, wg[cut, :])
        b = dot(flat, wu[cut, :])
        first = a if first is None else first + a
        second = b if second is None else second + b
    hidden = (first / (1.0 + jnp.exp(-first)) * second).astype(jnp.bfloat16)

    for c, cut in enumerate(cuts):
        down_in[c].wait()
        made = dot(hidden, wd[:, cut]).astype(jnp.bfloat16)
        part[:, :, cut] = made.reshape(experts, cap, size)
        for copy in giveback[c]:
            copy.start()
        ret[z, :, cut] = part[z, :, cut]

    for c, cut in enumerate(cuts):
        for copy in giveback[c]:
            copy.wait_recv()
        back = ret[:, :, cut].reshape(experts * cap, size)
        total = (dot(mix_hi, back) + dot(mix_lo, back)).astype(jnp.bfloat16)
        mixed[:, :, cut] = total.reshape(groups, own, size)
        for copy in scatter[c]:
            copy.start()
        red[g, :, cut] = mixed[g, :, cut]

    for c, cut in enumerate(cuts):
        for copy in scatter[c]:
            copy.wait_recv()
        out[:, cut] = jnp.sum(red[:, :, cut].astype(jnp.float32), axis=0).astype(jnp.bfloat16)

    for phase in (gather, dispatch, giveback, scatter):
        for copies in phase:
            for copy in copies:
                copy.wait_send()


def per_device(tokens, expert_ids, gate_codes, w_gate, w_up, w_down):
    groups = lax.axis_size("group")
    experts = lax.axis_size("expert")
    own, width = tokens.shape[1:]
    hid = w_gate.shape[2]
    bf16 = jnp.bfloat16
    any_space = pl.BlockSpec(memory_space=pl.ANY)
    dma = pltpu.SemaphoreType.DMA
    mixed = pl.pallas_call(
        functools.partial(kernel, groups, experts),
        out_shape=jax.ShapeDtypeStruct((own, width), bf16),
        in_specs=[any_space] * 6,
        out_specs=pl.BlockSpec(memory_space=pltpu.VMEM),
        scratch_shapes=[
            pltpu.VMEM((groups, own, width), bf16),
            pltpu.VMEM(expert_ids.shape[1:], jnp.int32),
            pltpu.VMEM(gate_codes.shape[1:], jnp.int32),
            pltpu.VMEM((width, hid), bf16),
            pltpu.VMEM((width, hid), bf16),
            pltpu.VMEM((hid, width), bf16),
            pltpu.VMEM((experts, CAPG, width), bf16),
            pltpu.VMEM((experts, CAPG, width), bf16),
            pltpu.VMEM((experts, CAPG, width), bf16),
            pltpu.VMEM((experts, CAPG, width), bf16),
            pltpu.VMEM((groups, own, width), bf16),
            pltpu.VMEM((groups, own, width), bf16),
            dma((3,)),
            dma((3, CHUNKS)),
            dma((CHUNKS, groups - 1)),
            dma((CHUNKS, groups - 1)),
            dma((CHUNKS, experts - 1)),
            dma((CHUNKS, experts - 1)),
            dma((CHUNKS, experts - 1)),
            dma((CHUNKS, experts - 1)),
            dma((CHUNKS, groups - 1)),
            dma((CHUNKS, groups - 1)),
        ],
        compiler_params=pltpu.CompilerParams(
            collective_id=0, has_side_effects=True, vmem_limit_bytes=60 * 1024 * 1024
        ),
    )(tokens[0], expert_ids[0], gate_codes[0], w_gate[0], w_up[0], w_down[0])
    return mixed[None]


def solution(mesh):
    placed = (
        P(("expert", "dp"), "group", None),
        P(("expert", "dp"), None, None),
        P(("expert", "dp"), None, None),
        P("expert", None, "group"),
        P("expert", None, "group"),
        P("expert", "group", None),
    )
    return jax.shard_map(
        per_device,
        mesh=mesh,
        in_specs=placed,
        out_specs=P(("expert", "dp"), "group", None),
        check_vma=False,
    )
```

time: 71.3 us -> 30.1 us (0.42)
  blocking collectives: 45.5 us -> 0 us
  Pallas kernels: 0 us -> 25.7 us
  matrix products: 12.1 us -> 0 us
  waiting for transfers between devices: 5.15 us -> 0 us
  starting transfers between devices: 3.38 us -> 0 us
  local copies, waits for them, and re-layouts: 3.28 us -> 4.17 us
  other arithmetic: 0.8 us -> 0 us
  between operations: 0.74 us -> 0.01 us
    pallas_call x0 -> x1, Pallas kernels: none -> 25.7 us  [per_device(): pl.pallas_call(functools.partial(kernel, groups, experts), out_shape=jax....]
    unnamed x1 -> x0, blocking collectives: 22.7 us -> none
    dot_general x4 -> x0, matrix products: 12.1 us -> none  [the longest x1 7.31 us: per_device(): jnp.dot(hidden, w_down[0], preferred_element_type=jnp.float32)]
    all_to_all x1 -> x0, blocking collectives: 11.6 us -> none  [per_device(): lax.all_to_all(rows, 'expert', split_axis=0, concat_axis=0, tiled=True)]
    all_gather x1 -> x0, blocking collectives: 11.3 us -> none  [per_device(): gathered = lax.all_gather(tokens, 'group', axis=1, tiled=True)]
    all_to_all x1 -> x0, waiting for transfers between devices: 5.15 us -> none  [per_device(): lax.all_to_all(partial_value, 'expert', split_axis=0, concat_axis=0, tile...]
    all_to_all x1 -> x0, starting transfers between devices: 3.38 us -> none  [per_device(): lax.all_to_all(partial_value, 'expert', split_axis=0, concat_axis=0, tile...]
    squeeze x0 -> x2, local copies, waits for them, and re-layouts: none -> 2.7 us  [the longest x1 1.35 us: per_device(): expert_ids[0]]
  transfers between devices with their start and end apart: 1 -> 0, of which waited for: 1 -> 0; matrix products, arithmetic and copies ran while one was open for 1% -> 0% of each run, Pallas kernels for 0% -> 0%
where the time goes in v1:
time: 30.1 us; the launch traced here: 29.9 us
  Pallas kernels  25.7 us (85%)
  local copies, waits for them, and re-layouts  4.17 us (14%)
    pallas_call x1, Pallas kernels, per_device(): pl.pallas_call(functools.partial(kernel, groups, experts), out_shape=jax....  25.7 us
    unnamed x1, local copies, waits for them, and re-layouts  1.46 us
    squeeze x1, local copies, waits for them, and re-layouts, per_device(): expert_ids[0]  1.35 us
    squeeze x1, local copies, waits for them, and re-layouts, per_device(): gate_codes[0]  1.35 us

profile of v1, /device:TPU:0, one launch (start us, length us, event | category | flops | bytes accessed | tf_op | source)
XLA Modules:
  0.0 29.9 jit_solution(3346064640476082422)
XLA Ops:
  0.0 1.4 %copy.7.ids = s32[16,8]{1,0:T(8,128)} copy(s32[16,8]{0,1:T(8,128)} %bitcast.12) | data formatting | bytes 1024 | tf_op jit(solution)/shard_map/squeeze | solution.py:227
  1.4 1.3 %copy.8.codes = s32[16,8]{1,0:T(8,128)} copy(s32[16,8]{0,1:T(8,128)} %bitcast.13) | data formatting | bytes 1024 | tf_op jit(solution)/shard_map/squeeze | solution.py:227
  2.7 25.7 %shard_map.64 = bf16[4,7168]{1,0:T(4,128)(2,1)} custom-call(bf16[4,7168]{1,0:T(4,128)(2,1)} %bitcast.11, s32[16,8]{1,0:T(8,128)} %copy.7.ids, s32[16,8]{1,0:T(8,128)} %copy.8.codes, bf16[7168,512]{1,0:T(8,128)(2,1)} %bitcast.7, bf16[7168,512]{1,0:T(8,128)(2,1)} %bitcast.8, bf16[512,7168]{1,0:T(8,128)(2,1)} %bitcast.9), custom_call_target="tpu_custom_call" | custom-call | tf_op jit(solution)/shard_map/pallas_call | solution.py:195
  28.4 1.5 %copy.10 = bf16[1,4,7168]{2,1,0:T(4,128)(2,1)} copy(bf16[1,4,7168]{2,1,0:T(4,128)(2,1)} %bitcast.10) | data formatting | bytes 114688

commit v2 on v1

v2 whole, which is shorter than its diff:
```python
import functools

import jax
import jax.numpy as jnp
from jax import lax
from jax.experimental import pallas as pl
from jax.experimental.pallas import tpu as pltpu
from jax.sharding import PartitionSpec as P

CAPG = 4
FORWARD = (1, 1, 1, 1)
BACK = (1, 1, 1, 1)
MESH = pl.DeviceIdType.MESH


def dot(a, b):
    return jnp.dot(a, b, preferred_element_type=jnp.float32)


def routing(ids, codes, experts, capacity):
    tokens = ids.shape[1]
    wide = experts * capacity
    codes = codes.astype(jnp.float32)
    gates = 2.5 * codes / jnp.sum(codes, axis=0, keepdims=True)
    slot = lax.broadcasted_iota(jnp.int32, (wide, tokens), 0)
    member = jnp.zeros((wide, tokens), jnp.float32)
    weight = jnp.zeros((wide, tokens), jnp.float32)
    for e in range(experts):
        hits = ids == e
        named = jnp.max(jnp.where(hits, 1.0, 0.0), axis=0, keepdims=True)
        gate = jnp.sum(jnp.where(hits, gates, 0.0), axis=0, keepdims=True)
        mine = (slot >= e * capacity) & (slot < (e + 1) * capacity)
        member = jnp.where(mine, named, member)
        weight = jnp.where(mine, gate, weight)
    row = lax.broadcasted_iota(jnp.int32, (tokens, tokens), 0)
    column = lax.broadcasted_iota(jnp.int32, (tokens, tokens), 1)
    before = jnp.where(row < column, 1.0, 0.0).astype(jnp.bfloat16)
    rank = dot(member.astype(jnp.bfloat16), before)
    place = jnp.where(rank == (slot % capacity).astype(jnp.float32), member, 0.0)
    return place, place * weight


def flipped(a):
    n = a.shape[1]
    row = lax.broadcasted_iota(jnp.int32, (n, n), 0)
    column = lax.broadcasted_iota(jnp.int32, (n, n), 1)
    eye = jnp.where(row == column, 1.0, 0.0).astype(jnp.bfloat16)
    return lax.dot_general(
        eye, a, (((1,), (1,)), ((), ())), preferred_element_type=jnp.float32
    ).astype(jnp.bfloat16)


def pieces(width, shares):
    ends = [0]
    for k in range(len(shares)):
        ends.append(width * sum(shares[: k + 1]) // sum(shares) // 128 * 128)
    return [pl.ds(a, b - a) for a, b in zip(ends[:-1], ends[1:])]


def kernel(
    groups, experts, tokens, ids, codes, w_gate, w_up, w_down, red,
    tok, ids_v, codes_v, wg, wu, wd, rows, slots, part, ret, mixed,
    in_sem, w_sem, d_sem, ga_s, ga_r, di_s, di_r, re_s, re_r, sc_s, sc_r, k_sem,
):
    g = lax.axis_index("group")
    z = lax.axis_index("expert")
    own = tokens.shape[0]
    width = tokens.shape[1]
    cuts = pieces(width, FORWARD)
    back_cuts = pieces(width, BACK)
    cap = CAPG

    tok_in = pltpu.make_async_copy(tokens, tok.at[g], in_sem.at[0])
    ids_in = pltpu.make_async_copy(ids, ids_v, in_sem.at[1])
    codes_in = pltpu.make_async_copy(codes, codes_v, in_sem.at[2])
    tok_in.start()
    ids_in.start()
    codes_in.start()

    barrier = pltpu.get_barrier_semaphore()
    group_peers = [lax.rem(g + k, groups) for k in range(1, groups)]
    expert_peers = [lax.rem(z + k, experts) for k in range(1, experts)]
    for peer in group_peers:
        pl.semaphore_signal(barrier, inc=1, device_id={"group": peer}, device_id_type=MESH)
    for peer in expert_peers:
        pl.semaphore_signal(barrier, inc=1, device_id={"expert": peer}, device_id_type=MESH)

    gate_in = [pltpu.make_async_copy(w_gate.at[cut, :], wg.at[cut, :], w_sem.at[0, c]) for c, cut in enumerate(cuts)]
    up_in = [pltpu.make_async_copy(w_up.at[cut, :], wu.at[cut, :], w_sem.at[1, c]) for c, cut in enumerate(cuts)]
    down_in = [pltpu.make_async_copy(w_down.at[:, cut], wd.at[:, cut], d_sem.at[c]) for c, cut in enumerate(back_cuts)]
    for c in range(len(cuts)):
        gate_in[c].start()
        up_in[c].start()
    for c in range(len(back_cuts)):
        down_in[c].start()

    ids_in.wait()
    codes_in.wait()
    pick, mix = routing(ids_v[...], codes_v[...], experts, cap)
    pick = pick.astype(jnp.bfloat16)
    mix_hi = mix.astype(jnp.bfloat16)
    mix_lo = flipped((mix - mix_hi.astype(jnp.float32)).astype(jnp.bfloat16))
    mix_hi = flipped(mix_hi)
    tok_in.wait()
    pl.semaphore_wait(barrier, groups + experts - 2)

    def remote(axis, peer, src, dst, send, recv):
        return pltpu.make_async_remote_copy(
            src_ref=src, dst_ref=dst, send_sem=send, recv_sem=recv,
            device_id={axis: peer}, device_id_type=MESH,
        )

    gather = [
        [
            remote("group", peer, tok.at[g, :, cut], tok.at[g, :, cut], ga_s.at[c, k], ga_r.at[c, k])
            for k, peer in enumerate(group_peers)
        ]
        for c, cut in enumerate(cuts)
    ]
    dispatch = [
        [
            remote("expert", peer, rows.at[peer, :, cut], slots.at[z, :, cut], di_s.at[c, k], di_r.at[c, k])
            for k, peer in enumerate(expert_peers)
        ]
        for c, cut in enumerate(cuts)
    ]
    giveback = [
        [
            remote("expert", peer, part.at[peer, :, cut], ret.at[z, :, cut], re_s.at[c, k], re_r.at[c, k])
            for k, peer in enumerate(expert_peers)
        ]
        for c, cut in enumerate(back_cuts)
    ]
    scatter = [
        [
            remote("group", peer, mixed.at[peer, :, cut], red.at[g, :, cut], sc_s.at[c, k], sc_r.at[c, k])
            for k, peer in enumerate(group_peers)
        ]
        for c, cut in enumerate(back_cuts)
    ]

    for c in range(len(cuts)):
        for copy in gather[c]:
            copy.start()
    for c, cut in enumerate(cuts):
        for copy in gather[c]:
            copy.wait_recv()
        chosen = dot(pick, tok[:, :, cut].reshape(groups * own, cut.size)).astype(jnp.bfloat16)
        rows[:, :, cut] = chosen.reshape(experts, cap, cut.size)
        for copy in dispatch[c]:
            copy.start()
        slots[z, :, cut] = rows[z, :, cut]

    first = second = None
    for c, cut in enumerate(cuts):
        for copy in dispatch[c]:
            copy.wait_recv()
        gate_in[c].wait()
        up_in[c].wait()
        flat = slots[:, :, cut].reshape(experts * cap, cut.size)
        a = dot(flat, wg[cut, :])
        b = dot(flat, wu[cut, :])
        first = a if first is None else first + a
        second = b if second is None else second + b
    hidden = (first / (1.0 + jnp.exp(-first)) * second).astype(jnp.bfloat16)

    for c, cut in enumerate(back_cuts):
        down_in[c].wait()
        made = dot(hidden, wd[:, cut]).astype(jnp.bfloat16)
        part[:, :, cut] = made.reshape(experts, cap, cut.size)
        for copy in giveback[c]:
            copy.start()
        ret[z, :, cut] = part[z, :, cut]

    keep = []
    for c, cut in enumerate(back_cuts):
        for copy in giveback[c]:
            copy.wait_recv()
        back = ret[:, :, cut].reshape(experts * cap, cut.size)
        total = (dot(mix_hi, back) + dot(mix_lo, back)).astype(jnp.bfloat16)
        mixed[:, :, cut] = total.reshape(groups, own, cut.size)
        for copy in scatter[c]:
            copy.start()
        keep.append(pltpu.make_async_copy(mixed.at[g, :, cut], red.at[g, :, cut], k_sem.at[c]))
        keep[c].start()

    for c in range(len(back_cuts)):
        for copy in scatter[c]:
            copy.wait_recv()
        keep[c].wait()

    for phase in (gather, dispatch, giveback, scatter):
        for copies in phase:
            for copy in copies:
                copy.wait_send()


def per_device(tokens, expert_ids, gate_codes, w_gate, w_up, w_down):
    groups = lax.axis_size("group")
    experts = lax.axis_size("expert")
    own, width = tokens.shape[1:]
    hid = w_gate.shape[2]
    bf16 = jnp.bfloat16
    any_space = pl.BlockSpec(memory_space=pl.ANY)
    dma = pltpu.SemaphoreType.DMA
    shares = pl.pallas_call(
        functools.partial(kernel, groups, experts),
        out_shape=jax.ShapeDtypeStruct((groups, own, width), bf16),
        in_specs=[any_space] * 6,
        out_specs=any_space,
        scratch_shapes=[
            pltpu.VMEM((groups, own, width), bf16),
            pltpu.VMEM(expert_ids.shape[:0:-1], jnp.int32),
            pltpu.VMEM(gate_codes.shape[:0:-1], jnp.int32),
            pltpu.VMEM((width, hid), bf16),
            pltpu.VMEM((width, hid), bf16),
            pltpu.VMEM((hid, width), bf16),
            pltpu.VMEM((experts, CAPG, width), bf16),
            pltpu.VMEM((experts, CAPG, width), bf16),
            pltpu.VMEM((experts, CAPG, width), bf16),
            pltpu.VMEM((experts, CAPG, width), bf16),
            pltpu.VMEM((groups, own, width), bf16),
            dma((3,)),
            dma((2, len(FORWARD))),
            dma((len(BACK),)),
            dma((len(FORWARD), groups - 1)),
            dma((len(FORWARD), groups - 1)),
            dma((len(FORWARD), experts - 1)),
            dma((len(FORWARD), experts - 1)),
            dma((len(BACK), experts - 1)),
            dma((len(BACK), experts - 1)),
            dma((len(BACK), groups - 1)),
            dma((len(BACK), groups - 1)),
            dma((len(BACK),)),
        ],
        compiler_params=pltpu.CompilerParams(
            collective_id=0, has_side_effects=True, vmem_limit_bytes=60 * 1024 * 1024
        ),
    )(tokens[0], expert_ids[0].T, gate_codes[0].T, w_gate[0], w_up[0], w_down[0])
    total = shares[0].astype(jnp.float32)
    for k in range(1, groups):
        total = total + shares[k].astype(jnp.float32)
    return total.astype(bf16)[None]


def solution(mesh):
    placed = (
        P(("expert", "dp"), "group", None),
        P(("expert", "dp"), None, None),
        P(("expert", "dp"), None, None),
        P("expert", None, "group"),
        P("expert", None, "group"),
        P("expert", "group", None),
    )
    return jax.shard_map(
        per_device,
        mesh=mesh,
        in_specs=placed,
        out_specs=P(("expert", "dp"), "group", None),
        check_vma=False,
    )
```

time: 30.1 us -> 27 us (0.90)
  local copies, waits for them, and re-layouts: 4.17 us -> 0 us
  other arithmetic: 0 us -> 1.59 us
  Pallas kernels: 25.7 us -> 25.2 us
    squeeze x2 -> x0, local copies, waits for them, and re-layouts: 2.7 us -> none  [the longest x1 1.35 us: per_device(): expert_ids[0]]
    convert_element_type x0 -> x1, other arithmetic: none -> 1.59 us  [per_device(): return total.astype(bf16)[None]]
    unnamed x1 -> x0, local copies, waits for them, and re-layouts: 1.46 us -> none
    pallas_call x1, Pallas kernels: 25.7 us -> 25.2 us  [per_device(): pl.pallas_call(functools.partial(kernel, groups, experts), out_shape=jax....]
where the time goes in v2:
time: 27 us; the launch traced here: 26.8 us
  Pallas kernels  25.2 us (93%)
  other arithmetic  1.59 us (6%)
    pallas_call x1, Pallas kernels, per_device(): pl.pallas_call(functools.partial(kernel, groups, experts), out_shape=jax....  25.2 us
    convert_element_type x1, other arithmetic, per_device(): return total.astype(bf16)[None]  1.59 us

profile of v2, /device:TPU:0, one launch (start us, length us, event | category | flops | bytes accessed | tf_op | source)
XLA Modules:
  0.0 26.8 jit_solution(2785470622858854129)
XLA Ops:
  0.0 25.2 %shard_map.64 = bf16[4,4,7168]{2,1,0:T(4,128)(2,1)} custom-call(bf16[4,7168]{1,0:T(4,128)(2,1)} %bitcast.13, s32[8,16]{1,0:T(8,128)} %bitcast.14, s32[8,16]{1,0:T(8,128)} %bitcast.15, bf16[7168,512]{1,0:T(8,128)(2,1)} %bitcast.10, bf16[7168,512]{1,0:T(8,128)(2,1)} %bitcast.11, bf16[512,7168]{1,0:T(8,128)(2,1)} %bitcast.12), custom_call_target="tpu_custom_call" | custom-call | tf_op jit(solution)/shard_map/pallas_call | solution.py:206
  25.2 1.6 %add_convert_fusion = bf16[1,4,7168]{2,1,0:T(4,128)(2,1)} fusion(bf16[4,4,7168]{2,1,0:T(4,128)(2,1)} %shard_map.64), kind=kLoop, calls=%fused_computation | loop fusion | flops 229376 | bytes 286720 | tf_op jit(solution)/shard_map/convert_element_type | solution.py:243

commit v3 on v2

--- a/solution.py
+++ b/solution.py
@@ -8,6 +8,7 @@
 from jax.sharding import PartitionSpec as P
 
 CAPG = 4
+GATHER = (1, 1, 1, 1)
 FORWARD = (1, 1, 1, 1)
 BACK = (1, 1, 1, 1)
 MESH = pl.DeviceIdType.MESH
@@ -57,6 +58,17 @@
     return [pl.ds(a, b - a) for a, b in zip(ends[:-1], ends[1:])]
 
 
+def partners(me, count):
+    found = []
+    for k in range(count - 1, 0, -1):
+        peer, bit = 0, 1
+        while bit < count:
+            peer += lax.rem(me // bit + k // bit, 2) * bit
+            bit *= 2
+        found.append(peer)
+    return found
+
+
 def kernel(
     groups, experts, tokens, ids, codes, w_gate, w_up, w_down, red,
     tok, ids_v, codes_v, wg, wu, wd, rows, slots, part, ret, mixed,
@@ -66,6 +78,7 @@
     z = lax.axis_index("expert")
     own = tokens.shape[0]
     width = tokens.shape[1]
+    wide_cuts = pieces(width, GATHER)
     cuts = pieces(width, FORWARD)
     back_cuts = pieces(width, BACK)
     cap = CAPG
@@ -78,7 +91,7 @@
     codes_in.start()
 
     barrier = pltpu.get_barrier_semaphore()
-    group_peers = [lax.rem(g + k, groups) for k in range(1, groups)]
+    group_peers = partners(g, groups)
     expert_peers = [lax.rem(z + k, experts) for k in range(1, experts)]
     for peer in group_peers:
         pl.semaphore_signal(barrier, inc=1, device_id={"group": peer}, device_id_type=MESH)
@@ -88,20 +101,20 @@
     gate_in = [pltpu.make_async_copy(w_gate.at[cut, :], wg.at[cut, :], w_sem.at[0, c]) for c, cut in enumerate(cuts)]
     up_in = [pltpu.make_async_copy(w_up.at[cut, :], wu.at[cut, :], w_sem.at[1, c]) for c, cut in enumerate(cuts)]
     down_in = [pltpu.make_async_copy(w_down.at[:, cut], wd.at[:, cut], d_sem.at[c]) for c, cut in enumerate(back_cuts)]
+    ids_in.wait()
+    codes_in.wait()
+    tok_in.wait()
     for c in range(len(cuts)):
         gate_in[c].start()
         up_in[c].start()
     for c in range(len(back_cuts)):
         down_in[c].start()
 
-    ids_in.wait()
-    codes_in.wait()
     pick, mix = routing(ids_v[...], codes_v[...], experts, cap)
     pick = pick.astype(jnp.bfloat16)
     mix_hi = mix.astype(jnp.bfloat16)
     mix_lo = flipped((mix - mix_hi.astype(jnp.float32)).astype(jnp.bfloat16))
     mix_hi = flipped(mix_hi)
-    tok_in.wait()
     pl.semaphore_wait(barrier, groups + experts - 2)
 
     def remote(axis, peer, src, dst, send, recv):
@@ -115,7 +128,7 @@
             remote("group", peer, tok.at[g, :, cut], tok.at[g, :, cut], ga_s.at[c, k], ga_r.at[c, k])
             for k, peer in enumerate(group_peers)
         ]
-        for c, cut in enumerate(cuts)
+        for c, cut in enumerate(wide_cuts)
     ]
     dispatch = [
         [
@@ -139,12 +152,15 @@
         for c, cut in enumerate(back_cuts)
     ]
 
-    for c in range(len(cuts)):
-        for copy in gather[c]:
-            copy.start()
+    for copies in gather:
+        for copy in copies:
+            copy.start()
+    here = 0
     for c, cut in enumerate(cuts):
-        for copy in gather[c]:
-            copy.wait_recv()
+        while here < len(wide_cuts) and wide_cuts[here].start < cut.start + cut.size:
+            for copy in gather[here]:
+                copy.wait_recv()
+            here += 1
         chosen = dot(pick, tok[:, :, cut].reshape(groups * own, cut.size)).astype(jnp.bfloat16)
         rows[:, :, cut] = chosen.reshape(experts, cap, cut.size)
         for copy in dispatch[c]:
@@ -223,8 +239,8 @@
             dma((3,)),
             dma((2, len(FORWARD))),
             dma((len(BACK),)),
-            dma((len(FORWARD), groups - 1)),
-            dma((len(FORWARD), groups - 1)),
+            dma((len(GATHER), groups - 1)),
+            dma((len(GATHER), groups - 1)),
             dma((len(FORWARD), experts - 1)),
             dma((len(FORWARD), experts - 1)),
             dma((len(BACK), experts - 1)),

time: 27 us -> 27 us (level)
  no operation moved by 1% of the time
where the time goes in v3:
time: 27 us; the launch traced here: 26.8 us
  Pallas kernels  25.2 us (93%)
  other arithmetic  1.59 us (6%)
    pallas_call x1, Pallas kernels, per_device(): pl.pallas_call(functools.partial(kernel, groups, experts), out_shape=jax....  25.2 us
    convert_element_type x1, other arithmetic, per_device(): return total.astype(bf16)[None]  1.59 us

profile of v3, /device:TPU:0, one launch (start us, length us, event | category | flops | bytes accessed | tf_op | source)
XLA Modules:
  0.0 26.8 jit_solution(4967746018061517845)
XLA Ops:
  0.0 25.2 %shard_map.64 = bf16[4,4,7168]{2,1,0:T(4,128)(2,1)} custom-call(bf16[4,7168]{1,0:T(4,128)(2,1)} %bitcast.13, s32[8,16]{1,0:T(8,128)} %bitcast.14, s32[8,16]{1,0:T(8,128)} %bitcast.15, bf16[7168,512]{1,0:T(8,128)(2,1)} %bitcast.10, bf16[7168,512]{1,0:T(8,128)(2,1)} %bitcast.11, bf16[512,7168]{1,0:T(8,128)(2,1)} %bitcast.12), custom_call_target="tpu_custom_call" | custom-call | tf_op jit(solution)/shard_map/pallas_call | solution.py:222
  25.2 1.6 %add_convert_fusion = bf16[1,4,7168]{2,1,0:T(4,128)(2,1)} fusion(bf16[4,4,7168]{2,1,0:T(4,128)(2,1)} %shard_map.64), kind=kLoop, calls=%fused_computation | loop fusion | flops 229376 | bytes 286720 | tf_op jit(solution)/shard_map/convert_element_type | solution.py:259
